TPU v7x, 128 devices: a whole 4x4x4 slice. The times are simulated.
128 devices in a mesh: dp: 16 (over z, x), mp: 8 (over y, core).
Axes of the slice: x: 4, y: 4, z: 4, core: 2. Of those that a mesh axis runs over, the one named last changes fastest.
Arguments:
- gradients: bfloat16 [8, 3584, 14336], P(None, 'dp', 'mp'), may hold values from -60 to 60
- column_slot: int32 [8, 16], replicated, may hold values from 0 to 15, as said below
- left_roots: bfloat16 [16, 8, 4, 896, 896], P('dp', 'mp'), may hold values from -1 to 5
- right_roots: bfloat16 [16, 8, 4, 896, 896], P('dp', 'mp'), may hold values from -1 to 5
Outputs:
- update: bfloat16 [8, 3584, 14336], P(None, 'dp', 'mp')
- clip_scale: float32 [], replicated
Inputs may be any that keep to these rules, and one draw needn't show every extreme that they name: `column_slot`: block column c belongs to group c // 2; over all matrices, the entries of one group's block columns are a permutation of 0 to 15.
All inputs are finite; a program needn't handle non-finite values.
Results may differ from a plain program's by a relative error of at most 0.0049.
Values may be sent and summed in bfloat16 or wider, within the bound.
A program may use at most 128 MiB of HBM per device.

v0:
```python
import functools

import jax
import jax.numpy as jnp
from jax import lax
from jax.experimental import pallas as pl
from jax.experimental.pallas import tpu as pltpu
from jax.sharding import PartitionSpec as P

D = 3584
FF = 14336
BLOCK = 896
MATRICES = 8
ROW_BLOCKS = 4
ROWS = 224
N_DP = 16
N_MP = 8
COLS = 2
SLOTS = 16
PART = 56
PARTS = ROWS // PART
SENT_WINDOW = 4
LEAD = 0
DEPUTY = 1
ORDER = "RRNRNRNN" + "RRRNRNNN"
PLAN = "1 2 3 L 4 5 6 7 T C D 8 9 10 A B 11 12 13 14 15"
LIMIT = 0.25
EPSILON = 1e-6
MESH = pl.DeviceIdType.MESH


def offset(dz, dx):
    return (dz % 4) * 4 + dx % 4


NEAR = [offset(*o) for o in ((1, 0), (3, 0), (1, 1), (3, 3), (1, 3), (3, 1), (1, 2), (3, 2))]
REST = [offset(*o) for o in ((0, 1), (0, 3), (2, 0), (2, 1), (2, 3), (0, 2), (2, 2))]


def exchange_kernel(
    slot_table, gradients, left, right, ret, clip_out,
    slot, first, own, send, recv, lbuf, rbuf, inverse, acc, dp_sums, mp_sums, total_sum,
    entered, slot_sem, first_sem, own_sem, root_sem, sent_sem, came_sem, sum_send, sum_recv,
):
    me = lax.axis_index("dp")
    mp = lax.axis_index("mp")
    z, x = me // 4, me % 4
    leads = me == LEAD

    def device(k):
        return lax.rem(z + k // 4, 4) * 4 + lax.rem(x + k % 4, 4)

    slot_copy = pltpu.make_async_copy(slot_table, slot, slot_sem)
    slot_copy.start()

    barrier = pltpu.get_barrier_semaphore()
    for k in range(1, N_DP):
        target = device(k)

        @pl.when(target != LEAD)
        def _(target=target):
            pl.semaphore_signal(barrier, inc=1, device_id={"dp": target}, device_id_type=MESH)

    @pl.when(leads)
    def _():
        for k in range(1, N_MP):
            pl.semaphore_signal(barrier, inc=1, device_id={"mp": lax.rem(mp + k, N_MP)}, device_id_type=MESH)

    def load(row, rows, dst, sems):
        copies = []
        for c in range(COLS):
            for m in range(MATRICES):
                j = c * MATRICES + m
                copy = pltpu.make_async_copy(
                    gradients.at[m, pl.ds(row, rows), pl.ds(c * BLOCK, BLOCK)],
                    dst.at[j, pl.ds(row, rows)],
                    sems.at[j],
                )
                copy.start()
                copies.append(copy)
        return copies

    first_loads = load(0, PART, first, first_sem)
    loads = load(PART, ROWS - PART, own, own_sem)
    slot_copy.wait()

    slots = [slot[m, mp * COLS + c] for c in range(COLS) for m in range(MATRICES)]
    for k in range(N_DP):
        target = device(k)
        found = jnp.int32(0)
        for j, value in enumerate(slots):
            found = jnp.where(value == target, jnp.int32(j), found)
        inverse[k] = found

    for copy in first_loads:
        copy.wait()

    acc[...] = jnp.zeros_like(acc)

    def stage(p, source):
        rows = pl.ds(p * PART, PART)
        total = acc[...]
        for k in range(N_DP):
            block = source[inverse[k], rows, :]
            if k == 0:
                recv[z, pl.ds(x * ROWS + p * PART, PART), :] = block
            else:
                send[k, rows, :] = block
            wide = block.astype(jnp.float32)
            square = wide * wide
            for lane in range(0, BLOCK, 128):
                total = total + square[:, lane : lane + 128]
        acc[...] = total

    def wait_rows(rows, sem):
        view = recv.at[0, pl.ds(0, rows)]
        pltpu.make_async_copy(view, view, sem).wait()

    def group(g):
        start = g - g % (2 * PARTS)
        return NEAR if ORDER[g] == "N" else REST, ORDER[start:g].count(ORDER[g])

    waited = {"sent": set(), "came": set()}

    def wait(kind, groups):
        sems = sent_sem if kind == "sent" else came_sem
        for g in groups:
            if g not in waited[kind]:
                wait_rows(len(group(g)[0]) * PART, sems.at[g])
                waited[kind].add(g)

    def issue(g):
        wait("sent", range(g + 1 - SENT_WINDOW))
        offsets, p = group(g)
        rows = pl.ds(p * PART, PART)
        for k in offsets:
            target = device(k)
            if g < 2 * PARTS:
                src, dst = send.at[k, rows], recv.at[z, pl.ds(x * ROWS + p * PART, PART)]
            else:
                src, dst = own.at[target, rows], ret.at[me, rows]
            pltpu.make_async_remote_copy(
                src_ref=src, dst_ref=dst, send_sem=sent_sem.at[g], recv_sem=came_sem.at[g],
                device_id={"dp": target}, device_id_type=MESH,
            ).start()

    stage(0, first)

    @pl.when(jnp.logical_not(leads))
    def _():
        pl.semaphore_wait(barrier, N_DP - 1)

    @pl.when(me == DEPUTY)
    def _():
        pl.semaphore_signal(entered, inc=1, device_id={"dp": LEAD}, device_id_type=MESH)

    @pl.when(leads)
    def _():
        pl.semaphore_wait(entered, 1)

    issue(0)
    for copy in loads:
        copy.wait()
    roots = []
    for r in range(ROW_BLOCKS):
        for h, (src, dst) in enumerate(((left, lbuf), (right, rbuf))):
            copy = pltpu.make_async_copy(src.at[0, 0, r], dst.at[r], root_sem.at[2 * r + h])
            copy.start()
            roots.append(copy)

    @pl.loop(1, PARTS)
    def _(p):
        stage(p, own)

    part = acc[...]
    dp_sums[me] = sum((part[i : i + 8] for i in range(8, PART, 8)), part[0:8])

    def to_lead():
        return pltpu.make_async_remote_copy(
            src_ref=dp_sums.at[me], dst_ref=dp_sums.at[me], send_sem=sum_send.at[0], recv_sem=sum_recv.at[0],
            device_id={"dp": LEAD}, device_id_type=MESH,
        )

    @pl.when(jnp.logical_not(leads))
    def _():
        to_lead().start()

    def wait_sums(ref, count, sem):
        view = ref.at[pl.ds(0, count)]
        pltpu.make_async_copy(view, view, sem).wait()

    def lead_sums():
        wait_sums(dp_sums, N_DP - 1, sum_recv.at[0])
        total = dp_sums[0]
        for i in range(1, N_DP):
            total = total + dp_sums[i]
        mp_sums[mp] = total
        pl.semaphore_wait(barrier, N_MP - 1)
        for k in range(1, N_MP):
            pltpu.make_async_remote_copy(
                src_ref=mp_sums.at[mp], dst_ref=mp_sums.at[mp], send_sem=sum_send.at[1], recv_sem=sum_recv.at[1],
                device_id={"mp": lax.rem(mp + k, N_MP)}, device_id_type=MESH,
            ).start()
        wait_sums(mp_sums, N_MP - 1, sum_send.at[1])
        wait_sums(mp_sums, N_MP - 1, sum_recv.at[1])
        total = mp_sums[0]
        for i in range(1, N_MP):
            total = total + mp_sums[i]
        total_sum[...] = total
        for k in range(1, N_DP):
            pltpu.make_async_remote_copy(
                src_ref=total_sum, dst_ref=total_sum, send_sem=sum_send.at[2], recv_sem=sum_recv.at[2],
                device_id={"dp": device(k)}, device_id_type=MESH,
            ).start()

    def finish_sums():
        @pl.when(jnp.logical_not(leads))
        def _():
            to_lead().wait_send()
            pltpu.make_async_copy(total_sum, total_sum, sum_recv.at[2]).wait()

        square_sum = jnp.broadcast_to(jnp.sum(total_sum[...], keepdims=True), (8, 128))
        clip = jnp.minimum(jnp.float32(1.0), LIMIT / jnp.sqrt(square_sum / (MATRICES * D * FF) + EPSILON))
        clip_out[...] = clip
        for copy in roots:
            copy.wait()

    def compute(dz):
        wait("came", [g for g in range(2 * PARTS) if ORDER[g] == ("N" if dz % 2 else "R")])
        r = lax.rem(z + 4 - dz, 4)
        scale = jnp.broadcast_to(clip_out[0:1, 0:1], (1, BLOCK))

        @pl.loop(0, 4)
        def _(i):
            product = jnp.dot(lbuf[r, pl.ds(i * ROWS, ROWS), :], recv[r], preferred_element_type=jnp.float32)
            scaled = (scale * product).astype(jnp.bfloat16)
            second = jnp.dot(scaled, rbuf[r], preferred_element_type=jnp.float32)
            own[r * 4 + i] = second.astype(jnp.bfloat16)

    for step in PLAN.split():
        if step.isdigit():
            issue(int(step))
        elif step == "L":
            pl.when(leads)(lead_sums)
        elif step == "T":
            finish_sums()
        else:
            compute({"A": 1, "B": 3, "C": 2, "D": 0}[step])
    ret[me] = own[me]
    wait("sent", range(4 * PARTS))
    wait("came", range(4 * PARTS))

    @pl.when(leads)
    def _():
        wait_sums(dp_sums, N_DP - 1, sum_send.at[2])


def place_kernel(slot, ret, clip, update, clip_out, clip_one, clip_sem, sem):
    mp = lax.axis_index("mp")
    clip_one[...] = clip[0:1, 0:1]
    clip_copy = pltpu.make_async_copy(clip_one, clip_out, clip_sem)
    clip_copy.start()
    copies = []
    for c in range(COLS):
        for m in range(MATRICES):
            copy = pltpu.make_async_copy(
                ret.at[slot[m, mp * COLS + c]], update.at[m, :, pl.ds(c * BLOCK, BLOCK)], sem.at[c * MATRICES + m]
            )
            copy.start()
            copies.append(copy)
    for copy in copies:
        copy.wait()
    clip_copy.wait()


def body(gradients, column_slot, left_roots, right_roots):
    block = (ROW_BLOCKS, BLOCK, BLOCK)
    columns = (SLOTS, ROWS, BLOCK)
    bf16, f32 = jnp.bfloat16, jnp.float32
    dma = pltpu.SemaphoreType.DMA
    anywhere = pl.BlockSpec(memory_space=pl.ANY)
    vmem = pl.BlockSpec(memory_space=pltpu.VMEM)
    smem = pl.BlockSpec(memory_space=pltpu.SMEM)
    ret, clip = pl.pallas_call(
        exchange_kernel,
        out_shape=(pltpu.VMEM(columns, bf16), pltpu.VMEM((8, 128), f32)),
        in_specs=[anywhere, anywhere, anywhere, anywhere],
        out_specs=(vmem, vmem),
        scratch_shapes=[
            pltpu.SMEM((MATRICES, COLS * N_MP), jnp.int32),
            pltpu.VMEM((SLOTS, PART, BLOCK), bf16),
            pltpu.VMEM(columns, bf16),
            pltpu.VMEM(columns, bf16),
            pltpu.VMEM(block, bf16),
            pltpu.VMEM(block, bf16),
            pltpu.VMEM(block, bf16),
            pltpu.SMEM((N_DP,), jnp.int32),
            pltpu.VMEM((PART, 128), f32),
            pltpu.VMEM((N_DP, 8, 128), f32),
            pltpu.VMEM((N_MP, 8, 128), f32),
            pltpu.VMEM((8, 128), f32),
            pltpu.SemaphoreType.REGULAR,
            dma,
            dma((COLS * MATRICES,)),
            dma((COLS * MATRICES,)),
            dma((2 * ROW_BLOCKS,)),
            dma((4 * PARTS,)),
            dma((4 * PARTS,)),
            dma((3,)),
            dma((3,)),
        ],
        compiler_params=pltpu.CompilerParams(
            collective_id=0, has_side_effects=True, vmem_limit_bytes=54 * 2**20
        ),
        name="exchange",
    )(column_slot, gradients, left_roots, right_roots)
    update, clip = pl.pallas_call(
        place_kernel,
        out_shape=(
            jax.ShapeDtypeStruct((MATRICES, ROWS, COLS * BLOCK), bf16),
            jax.ShapeDtypeStruct((1, 1), f32),
        ),
        in_specs=[smem, vmem, vmem],
        out_specs=(anywhere, anywhere),
        scratch_shapes=[pltpu.VMEM((1, 1), f32), dma, dma((COLS * MATRICES,))],
        compiler_params=pltpu.CompilerParams(vmem_limit_bytes=8 * 2**20),
        name="place",
    )(
        column_slot,
        pltpu.with_memory_space_constraint(ret, pltpu.VMEM),
        pltpu.with_memory_space_constraint(clip, pltpu.VMEM),
    )
    return update, clip[0, 0]


def solution(mesh):
    return jax.shard_map(
        body,
        mesh=mesh,
        in_specs=(P(None, "dp", "mp"), P(), P("dp", "mp"), P("dp", "mp")),
        out_specs=(P(None, "dp", "mp"), P()),
        check_vma=False,
    )
```

profile of v0, /device:TPU:0, one launch (start us, length us, event | category | flops | bytes accessed | tf_op | source)
XLA Modules:
  0.0 153.0 jit_solution(14129336703619960528)
XLA Ops:
  0.6 0.0 copy-start
  0.6 148.9 %exchange.1 = (bf16[16,224,896]{2,1,0:T(8,128)(2,1)S(1)}, f32[8,128]{1,0:T(8,128)S(1)}) custom-call(s32[8,16]{1,0:T(8,128)} %slot.1, bf16[8,224,1792]{2,1,0:T(8,128)(2,1)} %gradients.1, bf16[1,1,4,896,896]{4,3,2,1,0:T(8,128)(2,1)} %left.1, bf16[1,1,4,896,896]{4,3,2,1,0:T(8,128)(2,1)} %right.1), custom_call_target="tpu_custom_call" | custom-call | tf_op jit(solution)/shard_map/exchange/pallas_call | solution.py:284
  149.6 0.0 copy-done
  149.6 3.4 %place.1 = (bf16[8,224,1792]{2,1,0:T(8,128)(2,1)}, f32[1,1]{1,0:T(1,128)}) custom-call(s32[8,16]{1,0:T(8,128)S(1)} %copy-done, bf16[16,224,896]{2,1,0:T(8,128)(2,1)S(1)} %get-tuple-element.6.ret, f32[8,128]{1,0:T(8,128)S(1)} %get-tuple-element.7.clip), custom_call_target="tpu_custom_call" | custom-call | tf_op jit(solution)/shard_map/place/pallas_call | solution.py:317
Async XLA Ops:
  0.6 148.9 %copy-start = (s32[8,16]{1,0:T(8,128)S(1)}, s32[8,16]{1,0:T(8,128)}, u32[]{:S(2)}) copy-start(s32[8,16]{1,0:T(8,128)} %slot.1) | copy-start | bytes 1540
where the time goes:
time: 153 us
  Pallas kernels  152 us (99%)
    pallas_call x1, Pallas kernels, body(): pl.pallas_call(exchange_kernel, out_shape=(pltpu.VMEM(columns, bf16), plt...  149 us
    pallas_call x1, Pallas kernels, body(): pl.pallas_call(place_kernel, out_shape=(jax.ShapeDtypeStruct((MATRICES, R...  3.45 us

commit v1 on v0

--- a/solution.py
+++ b/solution.py
@@ -17,11 +17,15 @@
 N_MP = 8
 COLS = 2
 SLOTS = 16
-PART = 56
-PARTS = ROWS // PART
+SIZES = (56, 56, 56, 56)
+BACK_SIZES = (56, 56, 56, 56)
+PARTS = len(SIZES)
+FIRST = SIZES[0]
+STEP = SIZES[1]
+LANES = 56
 SENT_WINDOW = 4
-LEAD = 0
-DEPUTY = 1
+LEAD = 15
+DEPUTY = 14
 ORDER = "RRNRNRNN" + "RRRNRNNN"
 PLAN = "1 2 3 L 4 5 6 7 T C D 8 9 10 A B 11 12 13 14 15"
 LIMIT = 0.25
@@ -38,14 +42,16 @@
 
 
 def exchange_kernel(
-    slot_table, gradients, left, right, ret, clip_out,
+    slot_table, gradients, left, right, update, clip_out,
     slot, first, own, send, recv, lbuf, rbuf, inverse, acc, dp_sums, mp_sums, total_sum,
+    ret_0, ret_1, ret_2, ret_3,
     entered, slot_sem, first_sem, own_sem, root_sem, sent_sem, came_sem, sum_send, sum_recv,
 ):
     me = lax.axis_index("dp")
     mp = lax.axis_index("mp")
     z, x = me // 4, me % 4
     leads = me == LEAD
+    ret = (ret_0, ret_1, ret_2, ret_3)
 
     def device(k):
         return lax.rem(z + k // 4, 4) * 4 + lax.rem(x + k % 4, 4)
@@ -80,8 +86,7 @@
                 copies.append(copy)
         return copies
 
-    first_loads = load(0, PART, first, first_sem)
-    loads = load(PART, ROWS - PART, own, own_sem)
+    first_loads = load(0, FIRST, first, first_sem)
     slot_copy.wait()
 
     slots = [slot[m, mp * COLS + c] for c in range(COLS) for m in range(MATRICES)]
@@ -94,22 +99,24 @@
 
     for copy in first_loads:
         copy.wait()
+    loads = load(FIRST, ROWS - FIRST, own, own_sem)
 
     acc[...] = jnp.zeros_like(acc)
 
-    def stage(p, source):
-        rows = pl.ds(p * PART, PART)
+    def stage(start, size, source):
+        rows = pl.ds(start, size)
         total = acc[...]
         for k in range(N_DP):
             block = source[inverse[k], rows, :]
             if k == 0:
-                recv[z, pl.ds(x * ROWS + p * PART, PART), :] = block
+                recv[z, pl.ds(x * ROWS + start, size), :] = block
             else:
                 send[k, rows, :] = block
             wide = block.astype(jnp.float32)
             square = wide * wide
-            for lane in range(0, BLOCK, 128):
-                total = total + square[:, lane : lane + 128]
+            for row in range(0, size, LANES):
+                for lane in range(0, BLOCK, 128):
+                    total = total + square[row : row + LANES, lane : lane + 128]
         acc[...] = total
 
     def wait_rows(rows, sem):
@@ -118,7 +125,9 @@
 
     def group(g):
         start = g - g % (2 * PARTS)
-        return NEAR if ORDER[g] == "N" else REST, ORDER[start:g].count(ORDER[g])
+        sizes = SIZES if g < 2 * PARTS else BACK_SIZES
+        p = ORDER[start:g].count(ORDER[g])
+        return NEAR if ORDER[g] == "N" else REST, sum(sizes[:p]), sizes[p], p
 
     waited = {"sent": set(), "came": set()}
 
@@ -126,25 +135,26 @@
         sems = sent_sem if kind == "sent" else came_sem
         for g in groups:
             if g not in waited[kind]:
-                wait_rows(len(group(g)[0]) * PART, sems.at[g])
+                offsets, _, size, _ = group(g)
+                wait_rows(len(offsets) * size, sems.at[g])
                 waited[kind].add(g)
 
     def issue(g):
         wait("sent", range(g + 1 - SENT_WINDOW))
-        offsets, p = group(g)
-        rows = pl.ds(p * PART, PART)
+        offsets, start, size, p = group(g)
+        rows = pl.ds(start, size)
         for k in offsets:
             target = device(k)
             if g < 2 * PARTS:
-                src, dst = send.at[k, rows], recv.at[z, pl.ds(x * ROWS + p * PART, PART)]
+                src, dst = send.at[k, rows], recv.at[z, pl.ds(x * ROWS + start, size)]
             else:
-                src, dst = own.at[target, rows], ret.at[me, rows]
+                src, dst = own.at[target, rows], ret[p].at[me]
             pltpu.make_async_remote_copy(
                 src_ref=src, dst_ref=dst, send_sem=sent_sem.at[g], recv_sem=came_sem.at[g],
                 device_id={"dp": target}, device_id_type=MESH,
             ).start()
 
-    stage(0, first)
+    stage(0, FIRST, first)
 
     @pl.when(jnp.logical_not(leads))
     def _():
@@ -170,10 +180,10 @@
 
     @pl.loop(1, PARTS)
     def _(p):
-        stage(p, own)
+        stage(FIRST + (p - 1) * STEP, STEP, own)
 
     part = acc[...]
-    dp_sums[me] = sum((part[i : i + 8] for i in range(8, PART, 8)), part[0:8])
+    dp_sums[me] = sum((part[i : i + 8] for i in range(8, LANES, 8)), part[0:8])
 
     def to_lead():
         return pltpu.make_async_remote_copy(
@@ -246,31 +256,29 @@
             finish_sums()
         else:
             compute({"A": 1, "B": 3, "C": 2, "D": 0}[step])
-    ret[me] = own[me]
+    for p in range(PARTS):
+        start, size = sum(BACK_SIZES[:p]), BACK_SIZES[p]
+        rows = pl.ds(start, size)
+        ret[p][me] = own[me, rows, :]
+        wait("came", [g for g in range(2 * PARTS, 4 * PARTS) if group(g)[3] == p])
+        for c in range(COLS):
+            for m in range(MATRICES):
+                update[m, rows, pl.ds(c * BLOCK, BLOCK)] = ret[p][slot[m, mp * COLS + c]]
     wait("sent", range(4 * PARTS))
-    wait("came", range(4 * PARTS))
 
     @pl.when(leads)
     def _():
         wait_sums(dp_sums, N_DP - 1, sum_send.at[2])
 
 
-def place_kernel(slot, ret, clip, update, clip_out, clip_one, clip_sem, sem):
-    mp = lax.axis_index("mp")
+def place_kernel(columns, clip, update, clip_out, clip_one, clip_sem, sem):
     clip_one[...] = clip[0:1, 0:1]
-    clip_copy = pltpu.make_async_copy(clip_one, clip_out, clip_sem)
-    clip_copy.start()
-    copies = []
-    for c in range(COLS):
-        for m in range(MATRICES):
-            copy = pltpu.make_async_copy(
-                ret.at[slot[m, mp * COLS + c]], update.at[m, :, pl.ds(c * BLOCK, BLOCK)], sem.at[c * MATRICES + m]
-            )
-            copy.start()
-            copies.append(copy)
+    copies = [pltpu.make_async_copy(columns.at[m], update.at[m], sem.at[m]) for m in range(MATRICES)]
+    copies.append(pltpu.make_async_copy(clip_one, clip_out, clip_sem))
+    for copy in copies:
+        copy.start()
     for copy in copies:
         copy.wait()
-    clip_copy.wait()
 
 
 def body(gradients, column_slot, left_roots, right_roots):
@@ -280,25 +288,25 @@
     dma = pltpu.SemaphoreType.DMA
     anywhere = pl.BlockSpec(memory_space=pl.ANY)
     vmem = pl.BlockSpec(memory_space=pltpu.VMEM)
-    smem = pl.BlockSpec(memory_space=pltpu.SMEM)
     ret, clip = pl.pallas_call(
         exchange_kernel,
-        out_shape=(pltpu.VMEM(columns, bf16), pltpu.VMEM((8, 128), f32)),
+        out_shape=(pltpu.VMEM((MATRICES, ROWS, COLS * BLOCK), bf16), pltpu.VMEM((8, 128), f32)),
         in_specs=[anywhere, anywhere, anywhere, anywhere],
         out_specs=(vmem, vmem),
         scratch_shapes=[
             pltpu.SMEM((MATRICES, COLS * N_MP), jnp.int32),
-            pltpu.VMEM((SLOTS, PART, BLOCK), bf16),
+            pltpu.VMEM((SLOTS, FIRST, BLOCK), bf16),
             pltpu.VMEM(columns, bf16),
             pltpu.VMEM(columns, bf16),
             pltpu.VMEM(block, bf16),
             pltpu.VMEM(block, bf16),
             pltpu.VMEM(block, bf16),
             pltpu.SMEM((N_DP,), jnp.int32),
-            pltpu.VMEM((PART, 128), f32),
+            pltpu.VMEM((LANES, 128), f32),
             pltpu.VMEM((N_DP, 8, 128), f32),
             pltpu.VMEM((N_MP, 8, 128), f32),
             pltpu.VMEM((8, 128), f32),
+            *[pltpu.VMEM((SLOTS, size, BLOCK), bf16) for size in BACK_SIZES],
             pltpu.SemaphoreType.REGULAR,
             dma,
             dma((COLS * MATRICES,)),
@@ -320,13 +328,12 @@
             jax.ShapeDtypeStruct((MATRICES, ROWS, COLS * BLOCK), bf16),
             jax.ShapeDtypeStruct((1, 1), f32),
         ),
-        in_specs=[smem, vmem, vmem],
+        in_specs=[vmem, vmem],
         out_specs=(anywhere, anywhere),
-        scratch_shapes=[pltpu.VMEM((1, 1), f32), dma, dma((COLS * MATRICES,))],
+        scratch_shapes=[pltpu.VMEM((1, 1), f32), dma, dma((MATRICES,))],
         compiler_params=pltpu.CompilerParams(vmem_limit_bytes=8 * 2**20),
         name="place",
     )(
-        column_slot,
         pltpu.with_memory_space_constraint(ret, pltpu.VMEM),
         pltpu.with_memory_space_constraint(clip, pltpu.VMEM),
     )

time: 153 us -> 152 us (level)
  no operation moved by 1% of the time
where the time goes in v1:
time: 152 us; the launch traced here: 151 us
  Pallas kernels  151 us (99%)
    pallas_call x1, Pallas kernels, body(): pl.pallas_call(exchange_kernel, out_shape=(pltpu.VMEM((MATRICES, ROWS, CO...  148 us

profile of v1, /device:TPU:0, one launch (start us, length us, event | category | flops | bytes accessed | tf_op | source)
XLA Modules:
  0.0 151.4 jit_solution(9059032349605676727)
XLA Ops:
  0.6 147.9 %exchange.1 = (bf16[8,224,1792]{2,1,0:T(8,128)(2,1)S(1)}, f32[8,128]{1,0:T(8,128)S(1)}) custom-call(s32[8,16]{1,0:T(8,128)} %slot_table.1, bf16[8,224,1792]{2,1,0:T(8,128)(2,1)} %gradients.1, bf16[1,1,4,896,896]{4,3,2,1,0:T(8,128)(2,1)} %left.1, bf16[1,1,4,896,896]{4,3,2,1,0:T(8,128)(2,1)} %right.1), custom_call_target="tpu_custom_call" | custom-call | tf_op jit(solution)/shard_map/exchange/pallas_call | solution.py:291
  148.6 2.8 %place.1 = (bf16[8,224,1792]{2,1,0:T(8,128)(2,1)}, f32[1,1]{1,0:T(1,128)}) custom-call(bf16[8,224,1792]{2,1,0:T(8,128)(2,1)S(1)} %get-tuple-element.6.columns, f32[8,128]{1,0:T(8,128)S(1)} %get-tuple-element.7.clip), custom_call_target="tpu_custom_call" | custom-call | tf_op jit(solution)/shard_map/place/pallas_call | solution.py:325
